TPU v7x, 32 devices: a whole 2x2x4 slice. The times are simulated.
32 devices in a mesh: grp: 4 (over y, x), cp: 8 (over z, core).
Axes of the slice: x: 2, y: 2, z: 4, core: 2. Of those that a mesh axis runs over, the one named last changes fastest.
Arguments:
- queries: bfloat16 [16384, 2048], P(('grp', 'cp')), parts along dimension 0, may hold values from -6 to 6
- keys: bfloat16 [16384, 1024], P(('grp', 'cp')), parts along dimension 0, may hold values from -8 to 8
- values: bfloat16 [16384, 1024], P(('grp', 'cp')), parts along dimension 0, may hold values from -6 to 6
- doc_lengths: int32 [128], P('grp'), parts along dimension 0, may hold values from 1 to 1024, 4096 in all
Outputs:
- attended: bfloat16 [16384, 2048], P(('grp', 'cp')), parts along dimension 0
There are 4 independent parts, one for each index of `grp`. A program takes and returns all parts, laid end to end along the dimension named above; each array names one. Nothing has to cross between parts.
Inputs may be any that keep to these rules, and one draw needn't show every extreme that they name: doc_lengths sums to 4096, and its largest entry is exactly 1024.
All inputs are finite; a program needn't handle non-finite values.
Results may differ from a plain program's by a relative error of at most 0.0031.
Values may be sent and summed in bfloat16 or wider, within the bound.
A program may use at most 64 MiB of HBM per device.

v0:
```python
import jax
import jax.numpy as jnp
from jax import lax
from jax.sharding import PartitionSpec as P

HQ = 16
HK = 8
DH = 128
REACH = 2


query_scale = 144.0 ** (-0.5)


def shifted(block, axis, distance):
    devices = range(lax.axis_size(axis))
    route = [(i - distance, i) for i in devices if i - distance in devices]
    return lax.ppermute(block, axis, route)


def doc_index(positions, doc_ends):
    return jnp.sum((positions[:, None] >= doc_ends[None, :]).astype(jnp.int32), axis=1)


def on_device(queries, keys, values, doc_lengths):
    tok_rows = queries.shape[0]
    dev_index = lax.axis_index("cp")
    doc_ends = jnp.cumsum(doc_lengths)
    arrived = []
    passed = (keys, values)
    for offset in range(REACH):
        passed = shifted((passed[0], passed[1]), "cp", 1)
        arrived.append(passed)
    ordered = list(reversed(arrived)) + [(keys, values)]
    all_keys = jnp.concatenate([pair[0] for pair in ordered], axis=0)
    all_values = jnp.concatenate([pair[1] for pair in ordered], axis=0)
    first_row = dev_index * tok_rows
    query_pos = first_row + jnp.arange(tok_rows, dtype=jnp.int32)
    key_pos = first_row - REACH * tok_rows + jnp.arange(all_keys.shape[0], dtype=jnp.int32)
    same_doc = doc_index(query_pos, doc_ends)[:, None] == doc_index(key_pos, doc_ends)[None, :]
    visible = same_doc & (key_pos[None, :] <= query_pos[:, None]) & (key_pos[None, :] >= 0)
    groups = HQ // HK
    width = groups * DH

    def one_head(head, result):
        query_part = lax.dynamic_slice_in_dim(queries, head * width, width, 1).reshape(
            tok_rows, groups, DH
        )
        key_part = lax.dynamic_slice_in_dim(all_keys, head * DH, DH, 1)
        value_part = lax.dynamic_slice_in_dim(all_values, head * DH, DH, 1)
        scores = (
            jnp.einsum("tgd,wd->gtw", query_part, key_part, preferred_element_type=jnp.float32)
            * query_scale
        )
        scores = jnp.where(visible[None], scores, -jnp.inf)
        highest = jnp.max(scores, axis=-1, keepdims=True)
        weights = jnp.exp(scores - highest)
        totals = jnp.sum(weights, axis=-1)
        rounded = weights.astype(jnp.bfloat16)
        mixed = jnp.einsum("gtw,wd->tgd", rounded, value_part, preferred_element_type=jnp.float32)
        mixed = mixed / jnp.transpose(totals, (1, 0))[..., None]
        return lax.dynamic_update_slice_in_dim(
            result, mixed.reshape(tok_rows, width).astype(jnp.bfloat16), head * width, 1
        )

    return lax.fori_loop(0, HK, one_head, jnp.zeros_like(queries))


def solution(mesh):
    return jax.shard_map(
        on_device,
        mesh=mesh,
        in_specs=(P(("grp", "cp"), None), P(("grp", "cp"), None), P(("grp", "cp"), None), P("grp")),
        out_specs=P(("grp", "cp"), None),
        check_vma=False,
    )
```

profile of v0, /device:TPU:17, one launch (start us, length us, event | category | flops | bytes accessed | tf_op | source)
XLA Modules:
  0.0 132.3 jit_solution(11270513718010701818)
XLA Ops:
  0.0 1.6 %copy.19 = bf16[512,1024]{0,1:T(8,128)(2,1)S(1)} copy(bf16[512,1024]{1,0:T(8,128)(2,1)} %param.8) | data formatting | bytes 2097152 | tf_op args[2]
  1.6 3.8 %collective-permute-start = (bf16[512,1024]{0,1:T(8,128)(2,1)S(1)}, bf16[512,1024]{0,1:T(8,128)(2,1)}, u32[]{:S(2)}, u32[]{:S(2)}) collective-permute-start(bf16[512,1024]{0,1:T(8,128)(2,1)S(1)} %copy.19), channel_id=1, source_target_pairs={{0,1},{1,2},{2,3},{3,4},{4,5},{5,6},{6,7},{8,9},{9,10},{10,11},{11... | collective-permute-start | bytes 3145736 | tf_op jit(solution)/shard_map/ppermute | solution.py:18
  5.4 1.9 %collective-permute-start.2 = (bf16[512,1024]{1,0:T(8,128)(2,1)}, bf16[512,1024]{1,0:T(8,128)(2,1)S(1)}, u32[]{:S(2)}, u32[]{:S(2)}) collective-permute-start(bf16[512,1024]{1,0:T(8,128)(2,1)} %param.7), channel_id=1, source_target_pairs={{0,1},{1,2},{2,3},{3,4},{4,5},{5,6},{6,7},{8,9},{9,10},{10,11},{11... | collective-permute-start | bytes 3145736 | tf_op jit(solution)/shard_map/ppermute | solution.py:18
  7.3 9.8 %collective-permute-done = bf16[512,1024]{0,1:T(8,128)(2,1)} collective-permute-done((bf16[512,1024]{0,1:T(8,128)(2,1)S(1)}, bf16[512,1024]{0,1:T(8,128)(2,1)}, u32[]{:S(2)}, u32[]{:S(2)}) %collective-permute-start) | collective-permute-done | bytes 1048608 | tf_op jit(solution)/shard_map/ppermute | solution.py:18
  17.1 4.5 %collective-permute-start.1 = (bf16[512,1024]{0,1:T(8,128)(2,1)}, bf16[512,1024]{0,1:T(8,128)(2,1)}, u32[]{:S(2)}, u32[]{:S(2)}) collective-permute-start(bf16[512,1024]{0,1:T(8,128)(2,1)} %collective-permute-done), channel_id=1, source_target_pairs={{0,1},{1,2},{2,3},{3,4},{4,5},{5,6},{6,7},{8,9},{9,10},{10,11},{11... | collective-permute-start | bytes 3145736 | tf_op jit(solution)/shard_map/ppermute | solution.py:18
  21.6 6.8 %collective-permute-done.2 = bf16[512,1024]{1,0:T(8,128)(2,1)S(1)} collective-permute-done((bf16[512,1024]{1,0:T(8,128)(2,1)}, bf16[512,1024]{1,0:T(8,128)(2,1)S(1)}, u32[]{:S(2)}, u32[]{:S(2)}) %collective-permute-start.2) | collective-permute-done | bytes 1048608 | tf_op jit(solution)/shard_map/ppermute | solution.py:18
  28.4 4.3 %collective-permute-start.3 = (bf16[512,1024]{1,0:T(8,128)(2,1)S(1)}, bf16[512,1024]{1,0:T(8,128)(2,1)}, u32[]{:S(2)}, u32[]{:S(2)}) collective-permute-start(bf16[512,1024]{1,0:T(8,128)(2,1)S(1)} %collective-permute-done.2), channel_id=1, source_target_pairs={{0,1},{1,2},{2,3},{3,4},{4,5},{5,6},{6,7},{8,9},{9,10},{10,11},{11... | collective-permute-start | bytes 3145736 | tf_op jit(solution)/shard_map/ppermute | solution.py:18
  32.7 0.7 copy.21
  33.9 5.8 %collective-permute-done.1 = bf16[512,1024]{0,1:T(8,128)(2,1)} collective-permute-done((bf16[512,1024]{0,1:T(8,128)(2,1)}, bf16[512,1024]{0,1:T(8,128)(2,1)}, u32[]{:S(2)}, u32[]{:S(2)}) %collective-permute-start.1) | collective-permute-done | bytes 1048608 | tf_op jit(solution)/shard_map/ppermute | solution.py:18
  39.7 3.0 %pad_maximum_fusion = bf16[1536,1024]{0,1:T(8,128)(2,1)} fusion(bf16[512,1024]{0,1:T(8,128)(2,1)S(1)} %copy.19, bf16[512,1024]{0,1:T(8,128)(2,1)} %collective-permute-done, bf16[512,1024]{0,1:T(8,128)(2,1)} %collective-permute-done.1), kind=kLoop, calls=%fused_computation.23 | loop fusion | flops 9437184 | bytes 6291456 | tf_op jit(solution)/shard_map/concatenate | solution.py:36
  42.6 8.2 %collective-permute-done.3 = bf16[512,1024]{1,0:T(8,128)(2,1)} collective-permute-done((bf16[512,1024]{1,0:T(8,128)(2,1)S(1)}, bf16[512,1024]{1,0:T(8,128)(2,1)}, u32[]{:S(2)}, u32[]{:S(2)}) %collective-permute-start.3) | collective-permute-done | bytes 1048608 | tf_op jit(solution)/shard_map/ppermute | solution.py:18
  50.8 2.9 %pad_maximum_fusion.1 = bf16[1536,1024]{1,0:T(8,128)(2,1)} fusion(bf16[512,1024]{1,0:T(8,128)(2,1)S(1)} %copy-done.1, bf16[512,1024]{1,0:T(8,128)(2,1)S(1)} %collective-permute-done.2, bf16[512,1024]{1,0:T(8,128)(2,1)} %collective-permute-done.3), kind=kLoop, calls=%fused_computation.24 | loop fusion | flops 9437184 | bytes 6291456 | tf_op jit(solution)/shard_map/concatenate | solution.py:35
  53.7 0.2 broadcast_in_dim.45.clone
  54.0 77.0 %while.14 = (s32[]{:T(128)}, bf16[512,2048]{1,0:T(8,128)(2,1)S(1)}, bf16[1536,1024]{0,1:T(8,128)(2,1)}, bf16[1536,1024]{1,0:T(8,128)(2,1)}, bf16[512,2048]{1,0:T...) while((s32[]{:T(128)}, bf16[512,2048]{1,0:T(8,128)(2,1)S(1)}, ...), condition=%wide.region_6.7_spmd.clone, body=%wide.region_3.6_spmd.clone.sunk | while | flops 826013696 | bytes 25466632 | solution.py:66
  54.0 1.0 constant_dynamic-slice_fusion.2
  55.0 0.1 copy.31
  55.1 1.5 %and_and_fusion.2 = pred[512,1536]{0,1:T(8,128)(4,1)S(1)} fusion(s32[512]{0:T(512)S(1)} %get-tuple-element.288, s32[512]{0:T(512)S(1)} %get-tuple-element.287, s32[1536]{0:T(1024)S(1)} %get-tuple-element.289, s32[1536]{0:T(1024)S(1)} %get-tuple-element.286, pred[1536]{0:T(1024)(128)(4,1)S(1)} %get-tuple-element.290), kind=kLoop, calls=%fused_computation.7.clone.1 | loop fusion | flops 3145728 | bytes 804352 | tf_op jit(solution)/shard_map/and | solution.py:41
  56.6 2.3 %fusion.36 = (f32[2,512]{1,0:T(2,128)S(1)}, f32[1536,512,2]{1,0,2:T(8,128)S(1)}) fusion(pred[512,1536]{0,1:T(8,128)(4,1)S(1)} %and_and_fusion.2, bf16[512,2,128]{0,2,1:T(8,128)(2,1)S(1)} %bitcast.55, bf16[1536,1024]{1,0:T(8,128)(2,1)} %get-tuple-element.284, s32[]{:T(128)S(6)} %select_n.50), kind=kOutput, calls=%fused_computation.5.clone.1 | convolution fusion | flops 407370752 | bytes 7737348 | tf_op jit(solution)/shard_map/while/body/eval_jaxpr/tgd,wd->gtw/dot_general | solution.py:52
  59.0 1.4 %fusion.37 = f32[2,512]{1,0:T(2,128)S(1)} fusion(f32[1536,512,2]{1,0,2:T(8,128)S(1)} %get-tuple-element.247, f32[2,512]{1,0:T(2,128)S(1)} %get-tuple-element.248, pred[512,1536]{0,1:T(8,128)(4,1)S(1)} %and_and_fusion.2), kind=kLoop, calls=%fused_computation.3.clone.1 | loop fusion | flops 6290432 | bytes 7086080 | tf_op jit(solution)/shard_map/while/body/eval_jaxpr/reduce_sum | solution.py:58
  60.4 3.0 %fusion.38 = bf16[512,2,128]{0,2,1:T(8,128)(2,1)S(1)} fusion(f32[1536,512,2]{1,0,2:T(8,128)S(1)} %get-tuple-element.247, f32[2,512]{1,0:T(2,128)S(1)} %get-tuple-element.248, pred[512,1536]{0,1:T(8,128)(4,1)S(1)} %and_and_fusion.2, bf16[1536,1024]{0,1:T(8,128)(2,1)} %get-tuple-element.283, s32[]{:T(128)S(6)} %select_n.50, f32[512,2]{0,1:T(2,128)S(1)} %bitcast.56), kind=kOutput, calls=%fused_computation.11.clone.1 | convolution fusion | flops 409206784 | bytes 7741444 | tf_op jit(solution)/shard_map/while/body/eval_jaxpr/gtw,wd->tgd/dot_general | solution.py:60
  63.4 0.1 copy.32
  63.6 1.0 constant_dynamic-slice_fusion.2
  64.6 0.1 copy.31
  64.7 1.5 %and_and_fusion.2 = pred[512,1536]{0,1:T(8,128)(4,1)S(1)} fusion(s32[512]{0:T(512)S(1)} %get-tuple-element.288, s32[512]{0:T(512)S(1)} %get-tuple-element.287, s32[1536]{0:T(1024)S(1)} %get-tuple-element.289, s32[1536]{0:T(1024)S(1)} %get-tuple-element.286, pred[1536]{0:T(1024)(128)(4,1)S(1)} %get-tuple-element.290), kind=kLoop, calls=%fused_computation.7.clone.1 | loop fusion | flops 3145728 | bytes 804352 | tf_op jit(solution)/shard_map/and | solution.py:41
  66.3 2.3 %fusion.36 = (f32[2,512]{1,0:T(2,128)S(1)}, f32[1536,512,2]{1,0,2:T(8,128)S(1)}) fusion(pred[512,1536]{0,1:T(8,128)(4,1)S(1)} %and_and_fusion.2, bf16[512,2,128]{0,2,1:T(8,128)(2,1)S(1)} %bitcast.55, bf16[1536,1024]{1,0:T(8,128)(2,1)} %get-tuple-element.284, s32[]{:T(128)S(6)} %select_n.50), kind=kOutput, calls=%fused_computation.5.clone.1 | convolution fusion | flops 407370752 | bytes 7737348 | tf_op jit(solution)/shard_map/while/body/eval_jaxpr/tgd,wd->gtw/dot_general | solution.py:52
  68.6 1.4 %fusion.37 = f32[2,512]{1,0:T(2,128)S(1)} fusion(f32[1536,512,2]{1,0,2:T(8,128)S(1)} %get-tuple-element.247, f32[2,512]{1,0:T(2,128)S(1)} %get-tuple-element.248, pred[512,1536]{0,1:T(8,128)(4,1)S(1)} %and_and_fusion.2), kind=kLoop, calls=%fused_computation.3.clone.1 | loop fusion | flops 6290432 | bytes 7086080 | tf_op jit(solution)/shard_map/while/body/eval_jaxpr/reduce_sum | solution.py:58
  70.0 3.0 %fusion.38 = bf16[512,2,128]{0,2,1:T(8,128)(2,1)S(1)} fusion(f32[1536,512,2]{1,0,2:T(8,128)S(1)} %get-tuple-element.247, f32[2,512]{1,0:T(2,128)S(1)} %get-tuple-element.248, pred[512,1536]{0,1:T(8,128)(4,1)S(1)} %and_and_fusion.2, bf16[1536,1024]{0,1:T(8,128)(2,1)} %get-tuple-element.283, s32[]{:T(128)S(6)} %select_n.50, f32[512,2]{0,1:T(2,128)S(1)} %bitcast.56), kind=kOutput, calls=%fused_computation.11.clone.1 | convolution fusion | flops 409206784 | bytes 7741444 | tf_op jit(solution)/shard_map/while/body/eval_jaxpr/gtw,wd->tgd/dot_general | solution.py:60
  73.2 1.0 constant_dynamic-slice_fusion.2
  74.2 0.1 copy.31
  74.3 1.5 %and_and_fusion.2 = pred[512,1536]{0,1:T(8,128)(4,1)S(1)} fusion(s32[512]{0:T(512)S(1)} %get-tuple-element.288, s32[512]{0:T(512)S(1)} %get-tuple-element.287, s32[1536]{0:T(1024)S(1)} %get-tuple-element.289, s32[1536]{0:T(1024)S(1)} %get-tuple-element.286, pred[1536]{0:T(1024)(128)(4,1)S(1)} %get-tuple-element.290), kind=kLoop, calls=%fused_computation.7.clone.1 | loop fusion | flops 3145728 | bytes 804352 | tf_op jit(solution)/shard_map/and | solution.py:41
  75.9 2.3 %fusion.36 = (f32[2,512]{1,0:T(2,128)S(1)}, f32[1536,512,2]{1,0,2:T(8,128)S(1)}) fusion(pred[512,1536]{0,1:T(8,128)(4,1)S(1)} %and_and_fusion.2, bf16[512,2,128]{0,2,1:T(8,128)(2,1)S(1)} %bitcast.55, bf16[1536,1024]{1,0:T(8,128)(2,1)} %get-tuple-element.284, s32[]{:T(128)S(6)} %select_n.50), kind=kOutput, calls=%fused_computation.5.clone.1 | convolution fusion | flops 407370752 | bytes 7737348 | tf_op jit(solution)/shard_map/while/body/eval_jaxpr/tgd,wd->gtw/dot_general | solution.py:52
  78.2 1.4 %fusion.37 = f32[2,512]{1,0:T(2,128)S(1)} fusion(f32[1536,512,2]{1,0,2:T(8,128)S(1)} %get-tuple-element.247, f32[2,512]{1,0:T(2,128)S(1)} %get-tuple-element.248, pred[512,1536]{0,1:T(8,128)(4,1)S(1)} %and_and_fusion.2), kind=kLoop, calls=%fused_computation.3.clone.1 | loop fusion | flops 6290432 | bytes 7086080 | tf_op jit(solution)/shard_map/while/body/eval_jaxpr/reduce_sum | solution.py:58
  79.7 3.0 %fusion.38 = bf16[512,2,128]{0,2,1:T(8,128)(2,1)S(1)} fusion(f32[1536,512,2]{1,0,2:T(8,128)S(1)} %get-tuple-element.247, f32[2,512]{1,0:T(2,128)S(1)} %get-tuple-element.248, pred[512,1536]{0,1:T(8,128)(4,1)S(1)} %and_and_fusion.2, bf16[1536,1024]{0,1:T(8,128)(2,1)} %get-tuple-element.283, s32[]{:T(128)S(6)} %select_n.50, f32[512,2]{0,1:T(2,128)S(1)} %bitcast.56), kind=kOutput, calls=%fused_computation.11.clone.1 | convolution fusion | flops 409206784 | bytes 7741444 | tf_op jit(solution)/shard_map/while/body/eval_jaxpr/gtw,wd->tgd/dot_general | solution.py:60
  82.8 1.0 constant_dynamic-slice_fusion.2
  83.8 0.1 copy.31
  84.0 1.5 %and_and_fusion.2 = pred[512,1536]{0,1:T(8,128)(4,1)S(1)} fusion(s32[512]{0:T(512)S(1)} %get-tuple-element.288, s32[512]{0:T(512)S(1)} %get-tuple-element.287, s32[1536]{0:T(1024)S(1)} %get-tuple-element.289, s32[1536]{0:T(1024)S(1)} %get-tuple-element.286, pred[1536]{0:T(1024)(128)(4,1)S(1)} %get-tuple-element.290), kind=kLoop, calls=%fused_computation.7.clone.1 | loop fusion | flops 3145728 | bytes 804352 | tf_op jit(solution)/shard_map/and | solution.py:41
  85.5 2.3 %fusion.36 = (f32[2,512]{1,0:T(2,128)S(1)}, f32[1536,512,2]{1,0,2:T(8,128)S(1)}) fusion(pred[512,1536]{0,1:T(8,128)(4,1)S(1)} %and_and_fusion.2, bf16[512,2,128]{0,2,1:T(8,128)(2,1)S(1)} %bitcast.55, bf16[1536,1024]{1,0:T(8,128)(2,1)} %get-tuple-element.284, s32[]{:T(128)S(6)} %select_n.50), kind=kOutput, calls=%fused_computation.5.clone.1 | convolution fusion | flops 407370752 | bytes 7737348 | tf_op jit(solution)/shard_map/while/body/eval_jaxpr/tgd,wd->gtw/dot_general | solution.py:52
  87.8 1.4 %fusion.37 = f32[2,512]{1,0:T(2,128)S(1)} fusion(f32[1536,512,2]{1,0,2:T(8,128)S(1)} %get-tuple-element.247, f32[2,512]{1,0:T(2,128)S(1)} %get-tuple-element.248, pred[512,1536]{0,1:T(8,128)(4,1)S(1)} %and_and_fusion.2), kind=kLoop, calls=%fused_computation.3.clone.1 | loop fusion | flops 6290432 | bytes 7086080 | tf_op jit(solution)/shard_map/while/body/eval_jaxpr/reduce_sum | solution.py:58
  89.3 3.0 %fusion.38 = bf16[512,2,128]{0,2,1:T(8,128)(2,1)S(1)} fusion(f32[1536,512,2]{1,0,2:T(8,128)S(1)} %get-tuple-element.247, f32[2,512]{1,0:T(2,128)S(1)} %get-tuple-element.248, pred[512,1536]{0,1:T(8,128)(4,1)S(1)} %and_and_fusion.2, bf16[1536,1024]{0,1:T(8,128)(2,1)} %get-tuple-element.283, s32[]{:T(128)S(6)} %select_n.50, f32[512,2]{0,1:T(2,128)S(1)} %bitcast.56), kind=kOutput, calls=%fused_computation.11.clone.1 | convolution fusion | flops 409206784 | bytes 7741444 | tf_op jit(solution)/shard_map/while/body/eval_jaxpr/gtw,wd->tgd/dot_general | solution.py:60
  92.5 1.0 constant_dynamic-slice_fusion.2
  93.4 0.1 copy.31
  93.6 1.5 %and_and_fusion.2 = pred[512,1536]{0,1:T(8,128)(4,1)S(1)} fusion(s32[512]{0:T(512)S(1)} %get-tuple-element.288, s32[512]{0:T(512)S(1)} %get-tuple-element.287, s32[1536]{0:T(1024)S(1)} %get-tuple-element.289, s32[1536]{0:T(1024)S(1)} %get-tuple-element.286, pred[1536]{0:T(1024)(128)(4,1)S(1)} %get-tuple-element.290), kind=kLoop, calls=%fused_computation.7.clone.1 | loop fusion | flops 3145728 | bytes 804352 | tf_op jit(solution)/shard_map/and | solution.py:41
  95.1 2.3 %fusion.36 = (f32[2,512]{1,0:T(2,128)S(1)}, f32[1536,512,2]{1,0,2:T(8,128)S(1)}) fusion(pred[512,1536]{0,1:T(8,128)(4,1)S(1)} %and_and_fusion.2, bf16[512,2,128]{0,2,1:T(8,128)(2,1)S(1)} %bitcast.55, bf16[1536,1024]{1,0:T(8,128)(2,1)} %get-tuple-element.284, s32[]{:T(128)S(6)} %select_n.50), kind=kOutput, calls=%fused_computation.5.clone.1 | convolution fusion | flops 407370752 | bytes 7737348 | tf_op jit(solution)/shard_map/while/body/eval_jaxpr/tgd,wd->gtw/dot_general | solution.py:52
  97.5 1.4 %fusion.37 = f32[2,512]{1,0:T(2,128)S(1)} fusion(f32[1536,512,2]{1,0,2:T(8,128)S(1)} %get-tuple-element.247, f32[2,512]{1,0:T(2,128)S(1)} %get-tuple-element.248, pred[512,1536]{0,1:T(8,128)(4,1)S(1)} %and_and_fusion.2), kind=kLoop, calls=%fused_computation.3.clone.1 | loop fusion | flops 6290432 | bytes 7086080 | tf_op jit(solution)/shard_map/while/body/eval_jaxpr/reduce_sum | solution.py:58
  98.9 3.0 %fusion.38 = bf16[512,2,128]{0,2,1:T(8,128)(2,1)S(1)} fusion(f32[1536,512,2]{1,0,2:T(8,128)S(1)} %get-tuple-element.247, f32[2,512]{1,0:T(2,128)S(1)} %get-tuple-element.248, pred[512,1536]{0,1:T(8,128)(4,1)S(1)} %and_and_fusion.2, bf16[1536,1024]{0,1:T(8,128)(2,1)} %get-tuple-element.283, s32[]{:T(128)S(6)} %select_n.50, f32[512,2]{0,1:T(2,128)S(1)} %bitcast.56), kind=kOutput, calls=%fused_computation.11.clone.1 | convolution fusion | flops 409206784 | bytes 7741444 | tf_op jit(solution)/shard_map/while/body/eval_jaxpr/gtw,wd->tgd/dot_general | solution.py:60
  102.1 1.0 constant_dynamic-slice_fusion.2
  103.1 0.1 copy.31
  103.2 1.5 %and_and_fusion.2 = pred[512,1536]{0,1:T(8,128)(4,1)S(1)} fusion(s32[512]{0:T(512)S(1)} %get-tuple-element.288, s32[512]{0:T(512)S(1)} %get-tuple-element.287, s32[1536]{0:T(1024)S(1)} %get-tuple-element.289, s32[1536]{0:T(1024)S(1)} %get-tuple-element.286, pred[1536]{0:T(1024)(128)(4,1)S(1)} %get-tuple-element.290), kind=kLoop, calls=%fused_computation.7.clone.1 | loop fusion | flops 3145728 | bytes 804352 | tf_op jit(solution)/shard_map/and | solution.py:41
  104.8 2.3 %fusion.36 = (f32[2,512]{1,0:T(2,128)S(1)}, f32[1536,512,2]{1,0,2:T(8,128)S(1)}) fusion(pred[512,1536]{0,1:T(8,128)(4,1)S(1)} %and_and_fusion.2, bf16[512,2,128]{0,2,1:T(8,128)(2,1)S(1)} %bitcast.55, bf16[1536,1024]{1,0:T(8,128)(2,1)} %get-tuple-element.284, s32[]{:T(128)S(6)} %select_n.50), kind=kOutput, calls=%fused_computation.5.clone.1 | convolution fusion | flops 407370752 | bytes 7737348 | tf_op jit(solution)/shard_map/while/body/eval_jaxpr/tgd,wd->gtw/dot_general | solution.py:52
  107.1 1.4 %fusion.37 = f32[2,512]{1,0:T(2,128)S(1)} fusion(f32[1536,512,2]{1,0,2:T(8,128)S(1)} %get-tuple-element.247, f32[2,512]{1,0:T(2,128)S(1)} %get-tuple-element.248, pred[512,1536]{0,1:T(8,128)(4,1)S(1)} %and_and_fusion.2), kind=kLoop, calls=%fused_computation.3.clone.1 | loop fusion | flops 6290432 | bytes 7086080 | tf_op jit(solution)/shard_map/while/body/eval_jaxpr/reduce_sum | solution.py:58
  108.5 3.0 %fusion.38 = bf16[512,2,128]{0,2,1:T(8,128)(2,1)S(1)} fusion(f32[1536,512,2]{1,0,2:T(8,128)S(1)} %get-tuple-element.247, f32[2,512]{1,0:T(2,128)S(1)} %get-tuple-element.248, pred[512,1536]{0,1:T(8,128)(4,1)S(1)} %and_and_fusion.2, bf16[1536,1024]{0,1:T(8,128)(2,1)} %get-tuple-element.283, s32[]{:T(128)S(6)} %select_n.50, f32[512,2]{0,1:T(2,128)S(1)} %bitcast.56), kind=kOutput, calls=%fused_computation.11.clone.1 | convolution fusion | flops 409206784 | bytes 7741444 | tf_op jit(solution)/shard_map/while/body/eval_jaxpr/gtw,wd->tgd/dot_general | solution.py:60
  111.7 1.0 constant_dynamic-slice_fusion.2
  112.7 0.1 copy.31
  112.8 1.5 %and_and_fusion.2 = pred[512,1536]{0,1:T(8,128)(4,1)S(1)} fusion(s32[512]{0:T(512)S(1)} %get-tuple-element.288, s32[512]{0:T(512)S(1)} %get-tuple-element.287, s32[1536]{0:T(1024)S(1)} %get-tuple-element.289, s32[1536]{0:T(1024)S(1)} %get-tuple-element.286, pred[1536]{0:T(1024)(128)(4,1)S(1)} %get-tuple-element.290), kind=kLoop, calls=%fused_computation.7.clone.1 | loop fusion | flops 3145728 | bytes 804352 | tf_op jit(solution)/shard_map/and | solution.py:41
  114.4 2.3 %fusion.36 = (f32[2,512]{1,0:T(2,128)S(1)}, f32[1536,512,2]{1,0,2:T(8,128)S(1)}) fusion(pred[512,1536]{0,1:T(8,128)(4,1)S(1)} %and_and_fusion.2, bf16[512,2,128]{0,2,1:T(8,128)(2,1)S(1)} %bitcast.55, bf16[1536,1024]{1,0:T(8,128)(2,1)} %get-tuple-element.284, s32[]{:T(128)S(6)} %select_n.50), kind=kOutput, calls=%fused_computation.5.clone.1 | convolution fusion | flops 407370752 | bytes 7737348 | tf_op jit(solution)/shard_map/while/body/eval_jaxpr/tgd,wd->gtw/dot_general | solution.py:52
  116.7 1.4 %fusion.37 = f32[2,512]{1,0:T(2,128)S(1)} fusion(f32[1536,512,2]{1,0,2:T(8,128)S(1)} %get-tuple-element.247, f32[2,512]{1,0:T(2,128)S(1)} %get-tuple-element.248, pred[512,1536]{0,1:T(8,128)(4,1)S(1)} %and_and_fusion.2), kind=kLoop, calls=%fused_computation.3.clone.1 | loop fusion | flops 6290432 | bytes 7086080 | tf_op jit(solution)/shard_map/while/body/eval_jaxpr/reduce_sum | solution.py:58
  118.2 3.0 %fusion.38 = bf16[512,2,128]{0,2,1:T(8,128)(2,1)S(1)} fusion(f32[1536,512,2]{1,0,2:T(8,128)S(1)} %get-tuple-element.247, f32[2,512]{1,0:T(2,128)S(1)} %get-tuple-element.248, pred[512,1536]{0,1:T(8,128)(4,1)S(1)} %and_and_fusion.2, bf16[1536,1024]{0,1:T(8,128)(2,1)} %get-tuple-element.283, s32[]{:T(128)S(6)} %select_n.50, f32[512,2]{0,1:T(2,128)S(1)} %bitcast.56), kind=kOutput, calls=%fused_computation.11.clone.1 | convolution fusion | flops 409206784 | bytes 7741444 | tf_op jit(solution)/shard_map/while/body/eval_jaxpr/gtw,wd->tgd/dot_general | solution.py:60
  121.3 1.0 constant_dynamic-slice_fusion.2
  122.3 0.1 copy.31
  122.5 1.5 %and_and_fusion.2 = pred[512,1536]{0,1:T(8,128)(4,1)S(1)} fusion(s32[512]{0:T(512)S(1)} %get-tuple-element.288, s32[512]{0:T(512)S(1)} %get-tuple-element.287, s32[1536]{0:T(1024)S(1)} %get-tuple-element.289, s32[1536]{0:T(1024)S(1)} %get-tuple-element.286, pred[1536]{0:T(1024)(128)(4,1)S(1)} %get-tuple-element.290), kind=kLoop, calls=%fused_computation.7.clone.1 | loop fusion | flops 3145728 | bytes 804352 | tf_op jit(solution)/shard_map/and | solution.py:41
  124.0 2.3 %fusion.36 = (f32[2,512]{1,0:T(2,128)S(1)}, f32[1536,512,2]{1,0,2:T(8,128)S(1)}) fusion(pred[512,1536]{0,1:T(8,128)(4,1)S(1)} %and_and_fusion.2, bf16[512,2,128]{0,2,1:T(8,128)(2,1)S(1)} %bitcast.55, bf16[1536,1024]{1,0:T(8,128)(2,1)} %get-tuple-element.284, s32[]{:T(128)S(6)} %select_n.50), kind=kOutput, calls=%fused_computation.5.clone.1 | convolution fusion | flops 407370752 | bytes 7737348 | tf_op jit(solution)/shard_map/while/body/eval_jaxpr/tgd,wd->gtw/dot_general | solution.py:52
  126.3 1.4 %fusion.37 = f32[2,512]{1,0:T(2,128)S(1)} fusion(f32[1536,512,2]{1,0,2:T(8,128)S(1)} %get-tuple-element.247, f32[2,512]{1,0:T(2,128)S(1)} %get-tuple-element.248, pred[512,1536]{0,1:T(8,128)(4,1)S(1)} %and_and_fusion.2), kind=kLoop, calls=%fused_computation.3.clone.1 | loop fusion | flops 6290432 | bytes 7086080 | tf_op jit(solution)/shard_map/while/body/eval_jaxpr/reduce_sum | solution.py:58
  127.8 3.0 %fusion.38 = bf16[512,2,128]{0,2,1:T(8,128)(2,1)S(1)} fusion(f32[1536,512,2]{1,0,2:T(8,128)S(1)} %get-tuple-element.247, f32[2,512]{1,0:T(2,128)S(1)} %get-tuple-element.248, pred[512,1536]{0,1:T(8,128)(4,1)S(1)} %and_and_fusion.2, bf16[1536,1024]{0,1:T(8,128)(2,1)} %get-tuple-element.283, s32[]{:T(128)S(6)} %select_n.50, f32[512,2]{0,1:T(2,128)S(1)} %bitcast.56), kind=kOutput, calls=%fused_computation.11.clone.1 | convolution fusion | flops 409206784 | bytes 7741444 | tf_op jit(solution)/shard_map/while/body/eval_jaxpr/gtw,wd->tgd/dot_general | solution.py:60
  131.0 1.3 copy-done
  (25 shorter events, 1.5 us)
Async XLA Ops:
  0.0 50.8 %copy-start.1 = (bf16[512,1024]{1,0:T(8,128)(2,1)S(1)}, bf16[512,1024]{1,0:T(8,128)(2,1)}, u32[]{:S(2)}) copy-start(bf16[512,1024]{1,0:T(8,128)(2,1)} %param.7) | copy-start | bytes 3145732
  1.6 15.5 %collective-permute-start = (bf16[512,1024]{0,1:T(8,128)(2,1)S(1)}, bf16[512,1024]{0,1:T(8,128)(2,1)}, u32[]{:S(2)}, u32[]{:S(2)}) collective-permute-start(bf16[512,1024]{0,1:T(8,128)(2,1)S(1)} %copy.19), channel_id=1, source_target_pairs={{0,1},{1,2},{2,3},{3,4},{4,5},{5,6},{6,7},{8,9},{9,10},{10,11},{11... | collective-permute-start | bytes 3145736 | tf_op jit(solution)/shard_map/ppermute | solution.py:18
  5.4 23.1 %collective-permute-start.2 = (bf16[512,1024]{1,0:T(8,128)(2,1)}, bf16[512,1024]{1,0:T(8,128)(2,1)S(1)}, u32[]{:S(2)}, u32[]{:S(2)}) collective-permute-start(bf16[512,1024]{1,0:T(8,128)(2,1)} %param.7), channel_id=1, source_target_pairs={{0,1},{1,2},{2,3},{3,4},{4,5},{5,6},{6,7},{8,9},{9,10},{10,11},{11... | collective-permute-start | bytes 3145736 | tf_op jit(solution)/shard_map/ppermute | solution.py:18
  17.1 22.6 %collective-permute-start.1 = (bf16[512,1024]{0,1:T(8,128)(2,1)}, bf16[512,1024]{0,1:T(8,128)(2,1)}, u32[]{:S(2)}, u32[]{:S(2)}) collective-permute-start(bf16[512,1024]{0,1:T(8,128)(2,1)} %collective-permute-done), channel_id=1, source_target_pairs={{0,1},{1,2},{2,3},{3,4},{4,5},{5,6},{6,7},{8,9},{9,10},{10,11},{11... | collective-permute-start | bytes 3145736 | tf_op jit(solution)/shard_map/ppermute | solution.py:18
  28.4 22.4 %collective-permute-start.3 = (bf16[512,1024]{1,0:T(8,128)(2,1)S(1)}, bf16[512,1024]{1,0:T(8,128)(2,1)}, u32[]{:S(2)}, u32[]{:S(2)}) collective-permute-start(bf16[512,1024]{1,0:T(8,128)(2,1)S(1)} %collective-permute-done.2), channel_id=1, source_target_pairs={{0,1},{1,2},{2,3},{3,4},{4,5},{5,6},{6,7},{8,9},{9,10},{10,11},{11... | collective-permute-start | bytes 3145736 | tf_op jit(solution)/shard_map/ppermute | solution.py:18
  131.0 1.3 copy-start
where the time goes:
time: 134 us; the launch traced here: 132 us
  matrix products  42.5 us (32%)
  waiting for transfers between devices  30.6 us (23%)
  other arithmetic  30 us (22%)
  starting transfers between devices  14.4 us (11%)
  local copies, waits for them, and re-layouts  14.1 us (11%)
    ppermute x4, waiting for transfers between devices, shifted(): return lax.ppermute(block, axis, route)  30.6 us
    dot_general x8, matrix products, one_head(): jnp.einsum('gtw,wd->tgd', rounded, value_part, preferred_element_type=jnp...  23.9 us
    dot_general x8, matrix products, one_head(): jnp.einsum('tgd,wd->gtw', query_part, key_part, preferred_element_type=jn...  18.6 us
    ppermute x4, starting transfers between devices, shifted(): return lax.ppermute(block, axis, route)  14.4 us
    and x8, other arithmetic, on_device(): same_doc & (key_pos[None, :] <= query_pos[:, None])  12.2 us
    reduce_sum x8, other arithmetic, one_head(): totals = jnp.sum(weights, axis=-1)  11.5 us
    dynamic_slice x16, local copies, waits for them, and re-layouts, one_head(): lax.dynamic_slice_in_dim(queries, head * width, width, 1)  8.91 us
    concatenate x1, other arithmetic, on_device(): all_values = jnp.concatenate([pair[1] for pair in ordered], axis=0)  2.97 us
  transfers between devices with their start and end apart: 4, of which 4 were waited for; matrix products, arithmetic and copies ran while one was open for 3% of the time, Pallas kernels for 0%

commit v1 on v0

v1 whole, which is shorter than its diff:
```python
import functools
import math

import jax
import jax.numpy as jnp
from jax import lax
from jax.experimental import pallas as pl
from jax.experimental.pallas import tpu as pltpu
from jax.sharding import PartitionSpec as P

HQ = 16
HK = 8
DH = 128
REACH = 2
GROUPS = HQ // HK
WIDTH = GROUPS * DH
TILE = 128
MASKED = -1e30

exponent_scale = 144.0 ** (-0.5) * math.log2(math.e)


def kernel(
    shards,
    lengths_ref,
    queries_ref,
    keys_ref,
    values_ref,
    out_ref,
    held,
    query_held,
    out_held,
    bias,
    load_sem,
    query_sem,
    out_sem,
    chip_send,
    chip_recv,
    core_send,
    core_recv,
):
    me = lax.axis_index("cp")
    core = lax.rem(me, 2)
    partner = me + 1 - 2 * core
    rows = keys_ref.shape[0]
    docs = lengths_ref.shape[0]
    window = REACH * rows + TILE
    own = pl.ds(REACH * rows, rows)
    near = pl.ds(rows, rows)
    far = pl.ds(0, rows)
    has_prev = me >= 2
    has_next = me < shards - 2

    def loads(head):
        lanes = pl.ds(pl.multiple_of(head * DH, DH), DH)
        return (
            pltpu.make_async_copy(keys_ref.at[:, lanes], held.at[head, 0, own], load_sem.at[head, 0]),
            pltpu.make_async_copy(values_ref.at[:, lanes], held.at[head, 1, own], load_sem.at[head, 1]),
        )

    def query_load(head):
        lanes = pl.ds(pl.multiple_of(head * WIDTH, WIDTH), WIDTH)
        return pltpu.make_async_copy(queries_ref.at[:, lanes], query_held.at[head], query_sem.at[head])

    def out_store(head):
        lanes = pl.ds(pl.multiple_of(head * WIDTH, WIDTH), WIDTH)
        return pltpu.make_async_copy(out_held.at[head], out_ref.at[:, lanes], out_sem.at[head])

    def to_next_chip(head):
        return pltpu.make_async_remote_copy(
            src_ref=held.at[head, :, own],
            dst_ref=held.at[head, :, far],
            send_sem=chip_send.at[head],
            recv_sem=chip_recv.at[head],
            device_id={"cp": me + 2},
            device_id_type=pl.DeviceIdType.MESH,
        )

    def to_partner(head, source):
        return pltpu.make_async_remote_copy(
            src_ref=held.at[head, :, source],
            dst_ref=held.at[head, :, near],
            send_sem=core_send.at[head],
            recv_sem=core_recv.at[head],
            device_id={"cp": partner},
            device_id_type=pl.DeviceIdType.MESH,
        )

    @pl.loop(0, HK)
    def _(head):
        for copy in loads(head):
            copy.start()

    barrier = pltpu.get_barrier_semaphore()
    pl.semaphore_signal(barrier, inc=1, device_id={"cp": partner}, device_id_type=pl.DeviceIdType.MESH)

    @pl.when(has_prev)
    def _():
        pl.semaphore_signal(barrier, inc=1, device_id={"cp": me - 2}, device_id_type=pl.DeviceIdType.MESH)

    @pl.when(has_next)
    def _():
        pl.semaphore_signal(barrier, inc=1, device_id={"cp": me + 2}, device_id_type=pl.DeviceIdType.MESH)

    peers = 1 + jnp.where(has_prev, 1, 0) + jnp.where(has_next, 1, 0)
    pl.semaphore_wait(barrier, peers)

    @pl.loop(0, HK)
    def _(head):
        for copy in loads(head):
            copy.wait()

        @pl.when(has_next)
        def _():
            to_next_chip(head).start()

        @pl.when(core == 0)
        def _():
            to_partner(head, own).start()

    @pl.loop(0, HK)
    def _(head):
        query_load(head).start()

    @pl.when(jnp.logical_not(has_prev))
    def _():
        held[:, :, far, :] = jnp.zeros((HK, 2, rows, DH), held.dtype)

    @pl.when(me == 0)
    def _():
        held[:, :, near, :] = jnp.zeros((HK, 2, rows, DH), held.dtype)

    for tile in range(rows // TILE):
        query_pos = me * rows + tile * TILE + lax.broadcasted_iota(jnp.int32, (TILE, 1), 0)

        def next_doc(doc, state):
            end, begins = state
            end = end + lengths_ref[doc]
            return end, jnp.maximum(begins, jnp.where(query_pos >= end, end, 0))

        _, begins = lax.fori_loop(0, docs, next_doc, (jnp.int32(0), jnp.zeros((TILE, 1), jnp.int32)))
        key_pos = (
            (me - REACH) * rows + tile * TILE + lax.broadcasted_iota(jnp.int32, (TILE, window), 1)
        )
        visible = (key_pos >= begins) & (key_pos <= query_pos)
        bias[pl.ds(tile * TILE, TILE), :] = jnp.where(visible, 0.0, MASKED)

    @pl.loop(0, HK)
    def _(head):
        query_load(head).wait()

        @pl.when(has_prev)
        def _():
            to_next_chip(head).wait_recv()

            @pl.when(core == 1)
            def _():
                to_partner(head, far).start()

        @pl.when(me >= 1)
        def _():
            to_partner(head, far).wait_recv()

        for tile in range(rows // TILE):
            span = pl.ds(tile * TILE, TILE)
            queries = query_held[head, span, :]
            stacked = jnp.concatenate(
                [queries[:, g * DH : (g + 1) * DH] for g in range(GROUPS)], axis=0
            )
            scores = lax.dot_general(
                stacked,
                held[head, 0, pl.ds(tile * TILE, window), :],
                (((1,), (1,)), ((), ())),
                preferred_element_type=jnp.float32,
            )
            scores = scores.reshape(GROUPS, TILE, window) * exponent_scale + bias[span, :][None]
            highest = jnp.max(scores, axis=-1, keepdims=True)
            weights = jnp.exp2(scores - highest)
            totals = jnp.sum(weights, axis=-1, keepdims=True)
            mixed = jnp.dot(
                weights.astype(jnp.bfloat16).reshape(GROUPS * TILE, window),
                held[head, 1, pl.ds(tile * TILE, window), :],
                preferred_element_type=jnp.float32,
            ).reshape(GROUPS, TILE, DH)
            mixed = (mixed / totals).astype(jnp.bfloat16)
            for g in range(GROUPS):
                out_held[head, span, pl.ds(g * DH, DH)] = mixed[g]
        out_store(head).start()

    @pl.loop(0, HK)
    def _(head):
        out_store(head).wait()

        @pl.when(has_next)
        def _():
            to_next_chip(head).wait_send()

        @pl.when(jnp.logical_or(core == 0, has_prev))
        def _():
            to_partner(head, far).wait_send()


def on_device(queries, keys, values, doc_lengths):
    rows = keys.shape[0]
    shards = lax.axis_size("cp")
    window = REACH * rows + TILE
    return pl.pallas_call(
        functools.partial(kernel, shards),
        out_shape=jax.ShapeDtypeStruct(queries.shape, queries.dtype),
        in_specs=[
            pl.BlockSpec(memory_space=pltpu.SMEM),
            pl.BlockSpec(memory_space=pl.ANY),
            pl.BlockSpec(memory_space=pl.ANY),
            pl.BlockSpec(memory_space=pl.ANY),
        ],
        out_specs=pl.BlockSpec(memory_space=pl.ANY),
        scratch_shapes=[
            pltpu.VMEM((HK, 2, (REACH + 1) * rows, DH), keys.dtype),
            pltpu.VMEM((HK, rows, WIDTH), queries.dtype),
            pltpu.VMEM((HK, rows, WIDTH), queries.dtype),
            pltpu.VMEM((rows, window), jnp.float32),
            pltpu.SemaphoreType.DMA((HK, 2)),
            pltpu.SemaphoreType.DMA((HK,)),
            pltpu.SemaphoreType.DMA((HK,)),
            pltpu.SemaphoreType.DMA((HK,)),
            pltpu.SemaphoreType.DMA((HK,)),
            pltpu.SemaphoreType.DMA((HK,)),
            pltpu.SemaphoreType.DMA((HK,)),
        ],
        compiler_params=pltpu.CompilerParams(
            collective_id=0, has_side_effects=True, vmem_limit_bytes=48 * 1024 * 1024
        ),
    )(doc_lengths, queries, keys, values)


def solution(mesh):
    return jax.shard_map(
        on_device,
        mesh=mesh,
        in_specs=(P(("grp", "cp"), None), P(("grp", "cp"), None), P(("grp", "cp"), None), P("grp")),
        out_specs=P(("grp", "cp"), None),
        check_vma=False,
    )
```

time: 134 us -> 56.4 us (0.42)
  Pallas kernels: 0 us -> 50.9 us
  matrix products: 42.5 us -> 0 us
  waiting for transfers between devices: 30.6 us -> 0 us
  other arithmetic: 30 us -> 0 us
  starting transfers between devices: 14.4 us -> 0 us
  local copies, waits for them, and re-layouts: 14.1 us -> 4.42 us
    pallas_call x0 -> x1, Pallas kernels: none -> 50.9 us  [on_device(): pl.pallas_call(functools.partial(kernel, shards), out_shape=jax.ShapeDtyp...]
    dot_general x16 -> x0, matrix products: 42.5 us -> none  [the longest x8 23.9 us: one_head(): jnp.einsum('gtw,wd->tgd', rounded, value_part, preferred_element_type=jnp...]
    ppermute x4 -> x0, waiting for transfers between devices: 30.6 us -> none  [shifted(): return lax.ppermute(block, axis, route)]
    ppermute x4 -> x0, starting transfers between devices: 14.4 us -> none  [shifted(): return lax.ppermute(block, axis, route)]
    and x8 -> x0, other arithmetic: 12.2 us -> none  [on_device(): same_doc & (key_pos[None, :] <= query_pos[:, None])]
    reduce_sum x10 -> x0, other arithmetic: 11.7 us -> none  [the longest x8 11.5 us: one_head(): totals = jnp.sum(weights, axis=-1)]
    dynamic_slice x16 -> x0, local copies, waits for them, and re-layouts: 8.91 us -> none  [one_head(): lax.dynamic_slice_in_dim(queries, head * width, width, 1)]
    concatenate x2 -> x0, other arithmetic: 5.88 us -> none  [the longest x1 2.97 us: on_device(): all_values = jnp.concatenate([pair[1] for pair in ordered], axis=0)]
  transfers between devices with their start and end apart: 4 -> 0, of which waited for: 4 -> 0; matrix products, arithmetic and copies ran while one was open for 3% -> 0% of each run, Pallas kernels for 0% -> 0%
where the time goes in v1:
time: 56.4 us; the launch traced here: 55.3 us
  Pallas kernels  50.9 us (90%)
  local copies, waits for them, and re-layouts  4.42 us (8%)
    pallas_call x1, Pallas kernels, on_device(): pl.pallas_call(functools.partial(kernel, shards), out_shape=jax.ShapeDtyp...  50.9 us
    unnamed x7, local copies, waits for them, and re-layouts  4.42 us

profile of v1, /device:TPU:17, one launch (start us, length us, event | category | flops | bytes accessed | tf_op | source)
XLA Modules:
  0.0 55.3 jit_solution(15124069500785915855)
XLA Ops:
  0.0 0.0 copy-start
  0.0 1.2 %copy-done = bf16[512,1024]{1,0:T(8,128)(2,1)S(1)} copy-done((bf16[512,1024]{1,0:T(8,128)(2,1)S(1)}, bf16[512,1024]{1,0:T(8,128)(2,1)}, u32[]{:S(2)}) %copy-start) | copy-done | bytes 1048600
  1.2 0.0 copy-start.1
  1.2 1.2 %copy-done.1 = bf16[512,1024]{1,0:T(8,128)(2,1)S(1)} copy-done((bf16[512,1024]{1,0:T(8,128)(2,1)S(1)}, bf16[512,1024]{1,0:T(8,128)(2,1)}, u32[]{:S(2)}) %copy-start.1) | copy-done | bytes 1048600
  2.5 0.0 copy-start.2
  2.5 0.7 %copy-done.2 = s32[32]{0:T(128)S(1)} copy-done((s32[32]{0:T(128)S(1)}, s32[32]{0:T(128)}, u32[]{:S(2)}) %copy-start.2) | copy-done | bytes 152
  3.1 50.9 %shard_map.46 = bf16[512,2048]{1,0:T(8,128)(2,1)S(1)} custom-call(s32[32]{0:T(128)S(1)} %copy-done.2, bf16[512,2048]{1,0:T(8,128)(2,1)} %queries_ref.1, bf16[512,1024]{1,0:T(8,128)(2,1)S(1)} %copy-done, bf16[512,1024]{1,0:T(8,128)(2,1)S(1)} %copy-done.1), custom_call_target="tpu_custom_call" | custom-call | tf_op jit(solution)/shard_map/pallas_call | solution.py:207
  54.0 1.3 %copy.6 = bf16[512,2048]{1,0:T(8,128)(2,1)} copy(bf16[512,2048]{1,0:T(8,128)(2,1)S(1)} %shard_map.46) | data formatting | bytes 4194304
Async XLA Ops:
  0.0 1.2 %copy-start = (bf16[512,1024]{1,0:T(8,128)(2,1)S(1)}, bf16[512,1024]{1,0:T(8,128)(2,1)}, u32[]{:S(2)}) copy-start(bf16[512,1024]{1,0:T(8,128)(2,1)} %keys_ref.1) | copy-start | bytes 3145732
  1.2 1.2 %copy-start.1 = (bf16[512,1024]{1,0:T(8,128)(2,1)S(1)}, bf16[512,1024]{1,0:T(8,128)(2,1)}, u32[]{:S(2)}) copy-start(bf16[512,1024]{1,0:T(8,128)(2,1)} %values_ref.1) | copy-start | bytes 3145732
  2.5 0.7 %copy-start.2 = (s32[32]{0:T(128)S(1)}, s32[32]{0:T(128)}, u32[]{:S(2)}) copy-start(s32[32]{0:T(128)} %lengths_ref.1) | copy-start | bytes 388

commit v2 on v1

v2 whole, which is shorter than its diff:
```python
import functools
import math

import jax
import jax.numpy as jnp
from jax import lax
from jax.experimental import pallas as pl
from jax.experimental.pallas import tpu as pltpu
from jax.sharding import PartitionSpec as P

HQ = 16
HK = 8
DH = 128
REACH = 2
GROUPS = HQ // HK
WIDTH = GROUPS * DH
TILE = 128
MASKED = -1e30

exponent_scale = 144.0 ** (-0.5) * math.log2(math.e)


LOG2E = math.log2(math.e)
SPLIT = HK // 2
MESH = pl.DeviceIdType.MESH


def kernel(
    shards,
    lengths_ref,
    queries_ref,
    keys_ref,
    values_ref,
    out_ref,
    held,
    query_held,
    out_held,
    query_back,
    slot,
    stat_out,
    stat_in,
    bias,
    back_bias,
    load_sem,
    query_sem,
    out_sem,
    core_send,
    core_recv,
    query_send,
    query_recv,
    slot_send,
    slot_recv,
    relay_send,
    relay_recv,
    stat_send,
    stat_recv,
):
    me = lax.axis_index("cp")
    core = lax.rem(me, 2)
    even = core == 0
    odd = core == 1
    partner = me + 1 - 2 * core
    rows = keys_ref.shape[0]
    docs = lengths_ref.shape[0]
    tiles = rows // TILE
    window = REACH * rows + TILE
    own = pl.ds(REACH * rows, rows)
    near = pl.ds(rows, rows)
    far = pl.ds(0, rows)
    has_prev = me >= 2
    has_next = me < shards - 2
    chip_begin = (me - core) * rows
    next_begin = chip_begin + 2 * rows

    def loads(head):
        lanes = pl.ds(pl.multiple_of(head * DH, DH), DH)
        return (
            pltpu.make_async_copy(keys_ref.at[:, lanes], held.at[head, 0, own], load_sem.at[head, 0]),
            pltpu.make_async_copy(values_ref.at[:, lanes], held.at[head, 1, own], load_sem.at[head, 1]),
        )

    def query_load(head):
        lanes = pl.ds(pl.multiple_of(head * WIDTH, WIDTH), WIDTH)
        return pltpu.make_async_copy(queries_ref.at[:, lanes], query_held.at[head], query_sem.at[head])

    def out_store(head):
        lanes = pl.ds(pl.multiple_of(head * WIDTH, WIDTH), WIDTH)
        return pltpu.make_async_copy(out_held.at[head], out_ref.at[:, lanes], out_sem.at[head])

    def remote(source, target, send, recv, device):
        return pltpu.make_async_remote_copy(
            src_ref=source,
            dst_ref=target,
            send_sem=send,
            recv_sem=recv,
            device_id={"cp": device},
            device_id_type=MESH,
        )

    def to_core(head, region):
        return remote(
            held.at[head, :, own], held.at[head, :, region], core_send.at[head], core_recv.at[head], partner
        )

    def query_to_prev(step, side):
        return remote(
            query_held.at[side * SPLIT + step],
            query_back.at[step],
            query_send.at[side * SPLIT + step],
            query_recv.at[step],
            me - 2 + side,
        )

    def slot_to_next(step, region):
        return remote(
            slot.at[step],
            held.at[core * SPLIT + step, :, region],
            slot_send.at[step],
            slot_recv.at[step],
            me + 2,
        )

    def relay(step, source, target):
        head = core * SPLIT + step
        return remote(
            held.at[head, :, source], held.at[head, :, target], relay_send.at[step], relay_recv.at[step], partner
        )

    def stat_to_next(step, head):
        return remote(
            stat_out.at[step], stat_in.at[head], stat_send.at[step], stat_recv.at[head], me + 2 - core
        )

    @pl.loop(0, SPLIT)
    def _(step):
        query_load(step).start()
        query_load(SPLIT + step).start()

    @pl.loop(0, HK)
    def _(head):
        for copy in loads(head):
            copy.start()

    barrier = pltpu.get_barrier_semaphore()

    def greet(device):
        pl.semaphore_signal(barrier, inc=1, device_id={"cp": device}, device_id_type=MESH)

    greet(partner)

    @pl.when(has_prev)
    def _():
        greet(me - 2)

        @pl.when(even)
        def _():
            greet(me - 1)

    @pl.when(has_next)
    def _():
        greet(me + 2)

        @pl.when(odd)
        def _():
            greet(me + 1)

    back_peers = jnp.where(has_prev, 2 - core, 0)
    next_peers = jnp.where(has_next, 1 + core, 0)
    pl.semaphore_wait(barrier, 1 + back_peers + next_peers)

    @pl.loop(0, SPLIT)
    def _(step):
        for side in range(2):
            query_load(side * SPLIT + step).wait()

            @pl.when(jnp.logical_and(even, has_prev))
            def _():
                query_to_prev(step, side).start()

    @pl.loop(0, HK)
    def _(head):
        for copy in loads(head):
            copy.wait()

        @pl.when(even)
        def _():
            to_core(head, near).start()

        @pl.when(jnp.logical_and(odd, head < SPLIT))
        def _():
            to_core(head, far).start()

    @pl.when(jnp.logical_not(has_prev))
    def _():
        @pl.when(even)
        def _():
            held[:, :, near, :] = jnp.zeros((HK, 2, rows, DH), held.dtype)
            stat_in[...] = jnp.full(stat_in.shape, MASKED, jnp.float32)

        @pl.when(odd)
        def _():
            held[:, :, far, :] = jnp.zeros((HK, 2, rows, DH), held.dtype)

    def doc_begins(positions):
        def next_doc(doc, state):
            end, begins = state
            end = end + lengths_ref[doc]
            return end, jnp.maximum(begins, jnp.where(positions >= end, end, 0))

        start = (jnp.int32(0), jnp.zeros(positions.shape, jnp.int32))
        return lax.fori_loop(0, docs, next_doc, start)[1]

    def sends_keys(boundary):
        positions = jnp.full((1, DH), boundary, jnp.int32)
        return boundary - doc_begins(positions) <= rows

    row_iota = lax.broadcasted_iota(jnp.int32, (TILE, 1), 0)
    floor = jnp.where(sends_keys(chip_begin), 0, chip_begin)[:, :1]
    for tile in range(tiles):
        query_pos = me * rows + tile * TILE + row_iota
        begins = jnp.maximum(doc_begins(query_pos), floor)
        first = jnp.where(even, (me - 1) * rows, (me - 2) * rows + tile * TILE)
        key_pos = first + lax.broadcasted_iota(jnp.int32, (TILE, window), 1)
        visible = (key_pos >= begins) & (key_pos <= query_pos)
        bias[pl.ds(tile * TILE, TILE), :] = jnp.where(visible, 0.0, MASKED)

    for tile in range(tiles):
        begins = doc_begins(next_begin + tile * TILE + row_iota)
        key_pos = chip_begin + lax.broadcasted_iota(jnp.int32, (TILE, 2 * rows), 1)
        back_bias[pl.ds(tile * TILE, TILE), :] = jnp.where(key_pos >= begins, 0.0, MASKED)

    next_keys = sends_keys(next_begin)
    diagonal = lax.broadcasted_iota(jnp.int32, (TILE, TILE), 0) == lax.broadcasted_iota(
        jnp.int32, (TILE, TILE), 1
    )

    def stack(queries):
        return jnp.concatenate([queries[:, g * DH : (g + 1) * DH] for g in range(GROUPS)], axis=0)

    def dot_keys(queries, keys):
        return lax.dot_general(
            queries, keys, (((1,), (1,)), ((), ())), preferred_element_type=jnp.float32
        )

    def softmax(scores, mask):
        scores = scores.reshape(GROUPS, TILE, scores.shape[-1]) * exponent_scale + mask[None]
        highest = jnp.max(scores, axis=-1, keepdims=True)
        weights = jnp.exp2(scores - highest)
        totals = jnp.sum(weights, axis=-1, keepdims=True)
        rounded = weights.astype(jnp.bfloat16).reshape(GROUPS * TILE, scores.shape[-1])
        return highest, totals, rounded

    def dot_values(weights, values):
        return jnp.dot(weights, values, preferred_element_type=jnp.float32)

    def attend_back(step):
        head = core * SPLIT + step
        older = pl.multiple_of((2 - core) * rows, TILE)
        newer = pl.multiple_of(2 * core * rows, TILE)
        newer_rows = pl.ds(newer, rows)
        for tile in range(tiles):
            span = pl.ds(tile * TILE, TILE)
            count = rows - tile * TILE
            older_rows = pl.ds(older + tile * TILE, count)
            queries = stack(query_back[step, span, :])
            scores = jnp.concatenate(
                [
                    dot_keys(queries, held[head, 0, older_rows, :]),
                    dot_keys(queries, held[head, 0, newer_rows, :]),
                ],
                axis=1,
            )
            highest, totals, weights = softmax(scores, back_bias[span, pl.ds(tile * TILE, count + rows)])
            mixed = dot_values(weights[:, :count], held[head, 1, older_rows, :]) + dot_values(
                weights[:, count:], held[head, 1, newer_rows, :]
            )
            mixed = mixed.reshape(GROUPS, TILE, DH) / totals
            level = highest + jnp.log(totals) * LOG2E
            sent = pl.ds(newer + tile * TILE, TILE)
            for g in range(GROUPS):
                kept = held[head, g, sent, :].astype(jnp.float32)
                slot[step, g, span, :] = jnp.where(next_keys, kept, mixed[g]).astype(jnp.bfloat16)
                row = jnp.sum(jnp.where(diagonal, level[g], 0.0), axis=0, keepdims=True)
                stat_out[step, pl.ds(tile * GROUPS + g, 1), :] = jnp.where(next_keys, MASKED, row)

    def attend_even(head):
        for tile in range(tiles):
            span = pl.ds(tile * TILE, TILE)
            count = rows + (tile + 1) * TILE
            keys = pl.ds(rows, count)
            scores = dot_keys(stack(query_held[head, span, :]), held[head, 0, keys, :])
            highest, totals, weights = softmax(scores, bias[span, pl.ds(0, count)])
            mixed = dot_values(weights, held[head, 1, keys, :]).reshape(GROUPS, TILE, DH)
            for g in range(GROUPS):
                row = stat_in[head, pl.ds(tile * GROUPS + g, 1), :]
                level = jnp.sum(jnp.where(diagonal, row, 0.0), axis=1, keepdims=True)
                top = jnp.maximum(highest[g], level)
                here = jnp.exp2(highest[g] - top)
                there = jnp.exp2(level - top)
                partial = held[head, g, pl.ds(rows + tile * TILE, TILE), :].astype(jnp.float32)
                both = (mixed[g] * here + partial * there) / (totals[g] * here + there)
                out_held[head, span, pl.ds(g * DH, DH)] = both.astype(jnp.bfloat16)

    def attend_odd(head):
        for tile in range(tiles):
            span = pl.ds(tile * TILE, TILE)
            keys = pl.ds(tile * TILE, window)
            scores = dot_keys(stack(query_held[head, span, :]), held[head, 0, keys, :])
            _, totals, weights = softmax(scores, bias[span, :])
            mixed = dot_values(weights, held[head, 1, keys, :]).reshape(GROUPS, TILE, DH)
            mixed = (mixed / totals).astype(jnp.bfloat16)
            for g in range(GROUPS):
                out_held[head, span, pl.ds(g * DH, DH)] = mixed[g]

    @pl.when(even)
    def _():
        @pl.loop(0, SPLIT)
        def _(head):
            to_core(head, far).wait_recv()

    @pl.when(odd)
    def _():
        @pl.loop(0, HK)
        def _(head):
            to_core(head, near).wait_recv()

    @pl.loop(0, SPLIT + 1)
    def _(turn):
        @pl.when(jnp.logical_and(has_next, turn < SPLIT))
        def _():
            query_to_prev(turn, 0).wait_recv()
            attend_back(turn)

            @pl.when(even)
            def _():
                slot_to_next(turn, near).start()

            @pl.when(odd)
            def _():
                slot_to_next(turn, far).start()

            stat_to_next(turn, core * SPLIT + turn).start()

        @pl.when(turn >= 1)
        def _():
            step = turn - 1

            @pl.when(has_prev)
            def _():
                slot_to_next(step, far).wait_recv()

                @pl.when(even)
                def _():
                    relay(step, near, far).start()

                @pl.when(odd)
                def _():
                    relay(step, far, near).start()

            @pl.loop(0, 2)
            def _(turn_side):
                side = lax.rem(core + turn_side, 2)
                head = side * SPLIT + step

                @pl.when(jnp.logical_and(has_prev, turn_side == 1))
                def _():
                    relay(step, near, far).wait_recv()

                @pl.when(even)
                def _():
                    @pl.when(has_prev)
                    def _():
                        stat_to_next(step, head).wait_recv()

                    attend_even(head)

                @pl.when(odd)
                def _():
                    attend_odd(head)

                out_store(head).start()

    @pl.loop(0, HK)
    def _(head):
        out_store(head).wait()

        @pl.when(jnp.logical_or(even, head < SPLIT))
        def _():
            to_core(head, near).wait_send()

    @pl.loop(0, SPLIT)
    def _(step):
        @pl.when(has_next)
        def _():
            slot_to_next(step, near).wait_send()
            stat_to_next(step, step).wait_send()

        @pl.when(has_prev)
        def _():
            relay(step, near, far).wait_send()

            @pl.when(even)
            def _():
                for side in range(2):
                    query_to_prev(step, side).wait_send()


def on_device(queries, keys, values, doc_lengths):
    rows = keys.shape[0]
    shards = lax.axis_size("cp")
    window = REACH * rows + TILE
    stats = rows // TILE * GROUPS
    dma = pltpu.SemaphoreType.DMA
    return pl.pallas_call(
        functools.partial(kernel, shards),
        out_shape=jax.ShapeDtypeStruct(queries.shape, queries.dtype),
        in_specs=[
            pl.BlockSpec(memory_space=pltpu.SMEM),
            pl.BlockSpec(memory_space=pl.ANY),
            pl.BlockSpec(memory_space=pl.ANY),
            pl.BlockSpec(memory_space=pl.ANY),
        ],
        out_specs=pl.BlockSpec(memory_space=pl.ANY),
        scratch_shapes=[
            pltpu.VMEM((HK, 2, (REACH + 1) * rows, DH), keys.dtype),
            pltpu.VMEM((HK, rows, WIDTH), queries.dtype),
            pltpu.VMEM((HK, rows, WIDTH), queries.dtype),
            pltpu.VMEM((SPLIT, rows, WIDTH), queries.dtype),
            pltpu.VMEM((SPLIT, 2, rows, DH), keys.dtype),
            pltpu.VMEM((SPLIT, stats, TILE), jnp.float32),
            pltpu.VMEM((HK, stats, TILE), jnp.float32),
            pltpu.VMEM((rows, window), jnp.float32),
            pltpu.VMEM((rows, REACH * rows), jnp.float32),
            dma((HK, 2)),
            dma((HK,)),
            dma((HK,)),
            dma((HK,)),
            dma((HK,)),
            dma((HK,)),
            dma((SPLIT,)),
            dma((SPLIT,)),
            dma((SPLIT,)),
            dma((SPLIT,)),
            dma((SPLIT,)),
            dma((SPLIT,)),
            dma((HK,)),
        ],
        compiler_params=pltpu.CompilerParams(
            collective_id=0, has_side_effects=True, vmem_limit_bytes=58 * 1024 * 1024
        ),
    )(doc_lengths, queries, keys, values)


def solution(mesh):
    return jax.shard_map(
        on_device,
        mesh=mesh,
        in_specs=(P(("grp", "cp"), None), P(("grp", "cp"), None), P(("grp", "cp"), None), P("grp")),
        out_specs=P(("grp", "cp"), None),
        check_vma=False,
    )
```

time: 56.4 us -> 48.9 us (0.87)
  Pallas kernels: 50.9 us -> 45.1 us
  local copies, waits for them, and re-layouts: 4.42 us -> 3.16 us
    pallas_call x1, Pallas kernels: 50.9 us -> 45.1 us  [on_device(): pl.pallas_call(functools.partial(kernel, shards), out_shape=jax.ShapeDtyp...]
    unnamed x7 -> x1, local copies, waits for them, and re-layouts: 4.42 us -> 3.16 us
where the time goes in v2:
time: 48.9 us; the launch traced here: 48.3 us
  Pallas kernels  45.1 us (92%)
  local copies, waits for them, and re-layouts  3.16 us (6%)
    pallas_call x1, Pallas kernels, on_device(): pl.pallas_call(functools.partial(kernel, shards), out_shape=jax.ShapeDtyp...  45.1 us
    unnamed x1, local copies, waits for them, and re-layouts  3.16 us

profile of v2, /device:TPU:17, one launch (start us, length us, event | category | flops | bytes accessed | tf_op | source)
XLA Modules:
  0.0 48.3 jit_solution(24301821344553946)
XLA Ops:
  0.0 45.1 %shard_map.46 = bf16[512,2048]{1,0:T(8,128)(2,1)} custom-call(s32[32]{0:T(128)} %lengths_ref.1, bf16[512,2048]{1,0:T(8,128)(2,1)} %queries_ref.1, bf16[512,1024]{1,0:T(8,128)(2,1)} %keys_ref.1, bf16[512,1024]{1,0:T(8,128)(2,1)} %values_ref.1), custom_call_target="tpu_custom_call" | custom-call | tf_op jit(solution)/shard_map/pallas_call | solution.py:414
  45.1 3.2 %copy.6 = bf16[512,2048]{1,0:T(8,128)(2,1)} copy(bf16[512,2048]{1,0:T(8,128)(2,1)} %shard_map.46) | data formatting | bytes 4194304

commit v3 on v2

--- a/solution.py
+++ b/solution.py
@@ -41,6 +41,9 @@
     stat_in,
     bias,
     back_bias,
+    mixed_held,
+    highest_held,
+    totals_held,
     load_sem,
     query_sem,
     out_sem,
@@ -301,16 +304,50 @@
                 both = (mixed[g] * here + partial * there) / (totals[g] * here + there)
                 out_held[head, span, pl.ds(g * DH, DH)] = both.astype(jnp.bfloat16)
 
-    def attend_odd(head):
+    def attend_near(head):
         for tile in range(tiles):
             span = pl.ds(tile * TILE, TILE)
-            keys = pl.ds(tile * TILE, window)
+            skipped = rows - tile * TILE
+            count = window - skipped
+            keys = pl.ds(rows, count)
             scores = dot_keys(stack(query_held[head, span, :]), held[head, 0, keys, :])
-            _, totals, weights = softmax(scores, bias[span, :])
+            highest, totals, weights = softmax(scores, bias[span, pl.ds(skipped, count)])
             mixed = dot_values(weights, held[head, 1, keys, :]).reshape(GROUPS, TILE, DH)
-            mixed = (mixed / totals).astype(jnp.bfloat16)
+            mixed_held[head, :, span, :] = mixed
+            highest_held[head, :, span, :] = jnp.broadcast_to(highest, (GROUPS, TILE, DH))
+            totals_held[head, :, span, :] = jnp.broadcast_to(totals, (GROUPS, TILE, DH))
+
+    def attend_far(head):
+        for tile in range(tiles):
+            span = pl.ds(tile * TILE, TILE)
+            count = rows - tile * TILE
+            keys = pl.ds(tile * TILE, count)
+            scores = dot_keys(stack(query_held[head, span, :]), held[head, 0, keys, :])
+            highest, totals, weights = softmax(scores, bias[span, pl.ds(0, count)])
+            mixed = dot_values(weights, held[head, 1, keys, :]).reshape(GROUPS, TILE, DH)
+            earlier = highest_held[head, :, span, :]
+            top = jnp.maximum(highest, earlier)
+            here = jnp.exp2(highest - top)
+            there = jnp.exp2(earlier - top)
+            mixed = mixed * here + mixed_held[head, :, span, :] * there
+            mixed = mixed / (totals * here + totals_held[head, :, span, :] * there)
             for g in range(GROUPS):
-                out_held[head, span, pl.ds(g * DH, DH)] = mixed[g]
+                out_held[head, span, pl.ds(g * DH, DH)] = mixed[g].astype(jnp.bfloat16)
+
+    def attend_last(head):
+        @pl.when(even)
+        def _():
+            @pl.when(has_prev)
+            def _():
+                stat_to_next(0, head).wait_recv()
+
+            attend_even(head)
+
+        @pl.when(odd)
+        def _():
+            attend_far(head)
+
+        out_store(head).start()
 
     @pl.when(even)
     def _():
@@ -324,9 +361,12 @@
         def _(head):
             to_core(head, near).wait_recv()
 
-    @pl.loop(0, SPLIT + 1)
-    def _(turn):
-        @pl.when(jnp.logical_and(has_next, turn < SPLIT))
+    @pl.loop(0, HK + SPLIT + 2)
+    def _(count):
+        turn = count - 2
+        step = turn - 1
+
+        @pl.when(jnp.logical_and(has_next, jnp.logical_and(turn >= 0, turn < SPLIT)))
         def _():
             query_to_prev(turn, 0).wait_recv()
             attend_back(turn)
@@ -341,44 +381,34 @@
 
             stat_to_next(turn, core * SPLIT + turn).start()
 
-        @pl.when(turn >= 1)
-        def _():
-            step = turn - 1
-
-            @pl.when(has_prev)
-            def _():
-                slot_to_next(step, far).wait_recv()
-
-                @pl.when(even)
-                def _():
-                    relay(step, near, far).start()
-
-                @pl.when(odd)
-                def _():
-                    relay(step, far, near).start()
-
-            @pl.loop(0, 2)
-            def _(turn_side):
-                side = lax.rem(core + turn_side, 2)
-                head = side * SPLIT + step
-
-                @pl.when(jnp.logical_and(has_prev, turn_side == 1))
-                def _():
-                    relay(step, near, far).wait_recv()
-
-                @pl.when(even)
-                def _():
-                    @pl.when(has_prev)
-                    def _():
-                        stat_to_next(step, head).wait_recv()
-
-                    attend_even(head)
-
-                @pl.when(odd)
-                def _():
-                    attend_odd(head)
-
-                out_store(head).start()
+        @pl.when(jnp.logical_and(has_prev, jnp.logical_and(step >= 0, step < SPLIT)))
+        def _():
+            slot_to_next(step, far).wait_recv()
+
+            @pl.when(even)
+            def _():
+                relay(step, near, far).start()
+
+            @pl.when(odd)
+            def _():
+                relay(step, far, near).start()
+
+        @pl.when(jnp.logical_and(odd, count < HK))
+        def _():
+            attend_near(count)
+
+        done = count - 3 - core * (SPLIT - 1)
+
+        @pl.when(jnp.logical_and(done >= 0, done < HK))
+        def _():
+            relayed = lax.div(done, SPLIT)
+            step = lax.rem(done, SPLIT)
+
+            @pl.when(jnp.logical_and(has_prev, relayed == 1))
+            def _():
+                relay(step, near, far).wait_recv()
+
+            attend_last(lax.rem(core + relayed, 2) * SPLIT + step)
 
     @pl.loop(0, HK)
     def _(head):
@@ -416,9 +446,9 @@
         out_shape=jax.ShapeDtypeStruct(queries.shape, queries.dtype),
         in_specs=[
             pl.BlockSpec(memory_space=pltpu.SMEM),
-            pl.BlockSpec(memory_space=pl.ANY),
-            pl.BlockSpec(memory_space=pl.ANY),
-            pl.BlockSpec(memory_space=pl.ANY),
+            pl.BlockSpec(memory_space=pltpu.HBM),
+            pl.BlockSpec(memory_space=pltpu.HBM),
+            pl.BlockSpec(memory_space=pltpu.HBM),
         ],
         out_specs=pl.BlockSpec(memory_space=pl.ANY),
         scratch_shapes=[
@@ -431,6 +461,9 @@
             pltpu.VMEM((HK, stats, TILE), jnp.float32),
             pltpu.VMEM((rows, window), jnp.float32),
             pltpu.VMEM((rows, REACH * rows), jnp.float32),
+            pltpu.VMEM((HK, GROUPS, rows, DH), jnp.float32),
+            pltpu.VMEM((HK, GROUPS, rows, DH), jnp.float32),
+            pltpu.VMEM((HK, GROUPS, rows, DH), jnp.float32),
             dma((HK, 2)),
             dma((HK,)),
             dma((HK,)),

time: 48.9 us -> 53.5 us (1.094)
  Pallas kernels: 45.1 us -> 49.9 us
    pallas_call x1, Pallas kernels: 45.1 us -> 49.9 us  [on_device(): pl.pallas_call(functools.partial(kernel, shards), out_shape=jax.ShapeDtyp...]
where the time goes in v3:
time: 53.5 us; the launch traced here: 53.1 us
  Pallas kernels  49.9 us (93%)
  local copies, waits for them, and re-layouts  3.16 us (6%)
    pallas_call x1, Pallas kernels, on_device(): pl.pallas_call(functools.partial(kernel, shards), out_shape=jax.ShapeDtyp...  49.9 us
    unnamed x1, local copies, waits for them, and re-layouts  3.16 us

profile of v3, /device:TPU:17, one launch (start us, length us, event | category | flops | bytes accessed | tf_op | source)
XLA Modules:
  0.0 53.1 jit_solution(15408533239882326246)
XLA Ops:
  0.0 49.9 %shard_map.46 = bf16[512,2048]{1,0:T(8,128)(2,1)} custom-call(s32[32]{0:T(128)} %lengths_ref.1, bf16[512,2048]{1,0:T(8,128)(2,1)} %queries_ref.1, bf16[512,1024]{1,0:T(8,128)(2,1)} %keys_ref.1, bf16[512,1024]{1,0:T(8,128)(2,1)} %values_ref.1), custom_call_target="tpu_custom_call" | custom-call | tf_op jit(solution)/shard_map/pallas_call | solution.py:444
  49.9 3.2 %copy.6 = bf16[512,2048]{1,0:T(8,128)(2,1)} copy(bf16[512,2048]{1,0:T(8,128)(2,1)} %shard_map.46) | data formatting | bytes 4194304

commit v4 on v2

--- a/solution.py
+++ b/solution.py
@@ -133,8 +133,8 @@
 
     @pl.loop(0, SPLIT)
     def _(step):
+        query_load(SPLIT + step).start()
         query_load(step).start()
-        query_load(SPLIT + step).start()
 
     @pl.loop(0, HK)
     def _(head):
@@ -170,7 +170,7 @@
 
     @pl.loop(0, SPLIT)
     def _(step):
-        for side in range(2):
+        for side in (1, 0):
             query_load(side * SPLIT + step).wait()
 
             @pl.when(jnp.logical_and(even, has_prev))

time: 48.9 us -> 49 us (level)
  Pallas kernels: 45.1 us -> 45.6 us
    pallas_call x1, Pallas kernels: 45.1 us -> 45.6 us  [on_device(): pl.pallas_call(functools.partial(kernel, shards), out_shape=jax.ShapeDtyp...]
where the time goes in v4:
time: 49 us; the launch traced here: 48.8 us
  Pallas kernels  45.6 us (93%)
  local copies, waits for them, and re-layouts  3.16 us (6%)
    pallas_call x1, Pallas kernels, on_device(): pl.pallas_call(functools.partial(kernel, shards), out_shape=jax.ShapeDtyp...  45.6 us
    unnamed x1, local copies, waits for them, and re-layouts  3.16 us

profile of v4, /device:TPU:17, one launch (start us, length us, event | category | flops | bytes accessed | tf_op | source)
XLA Modules:
  0.0 48.8 jit_solution(6397463159095847481)
XLA Ops:
  0.0 45.6 %shard_map.46 = bf16[512,2048]{1,0:T(8,128)(2,1)} custom-call(s32[32]{0:T(128)} %lengths_ref.1, bf16[512,2048]{1,0:T(8,128)(2,1)} %queries_ref.1, bf16[512,1024]{1,0:T(8,128)(2,1)} %keys_ref.1, bf16[512,1024]{1,0:T(8,128)(2,1)} %values_ref.1), custom_call_target="tpu_custom_call" | custom-call | tf_op jit(solution)/shard_map/pallas_call | solution.py:414
  45.6 3.2 %copy.6 = bf16[512,2048]{1,0:T(8,128)(2,1)} copy(bf16[512,2048]{1,0:T(8,128)(2,1)} %shard_map.46) | data formatting | bytes 4194304
